TPU v7x, 512 devices: a 4x2x32 block of a 4x8x32 slice. The times are simulated.
512 devices in a mesh: parts: 2 (over y), seq: 32 (over z), head: 8 (over x, core).
Axes of the slice: x: 4, y: 2, z: 32, core: 2. Of those that a mesh axis runs over, the one named last changes fastest.
The devices are a block of a 4x8x32 slice.
Arguments:
- hidden: bfloat16 [48, 12288], P(('parts', 'head'), 'seq'), parts along dimension 0, may hold values from -600 to 600
- norm_gain: float32 [12288], P('seq'), may hold values from 0.1 to 1.9
- w_query: bfloat16 [12288, 12288], P('seq', 'head'), may hold values from -0.0546875 to 0.0546875
- w_key: bfloat16 [12288, 1024], P('seq', 'head'), may hold values from -0.0546875 to 0.0546875
- w_value: bfloat16 [12288, 1024], P('seq', 'head'), may hold values from -0.0546875 to 0.0546875
- w_out: bfloat16 [12288, 12288], P('head', 'seq'), may hold values from -0.0546875 to 0.0546875
- lengths: int32 [48], P('parts'), parts along dimension 0, may hold values from 1 to 4096, as said below
- key_cache: bfloat16 [48, 8, 4096, 128], P('parts', 'head', 'seq'), parts along dimension 0, may hold values from -600 to 600, as said below
- value_cache: bfloat16 [48, 8, 4096, 128], P('parts', 'head', 'seq'), parts along dimension 0, may hold values from -6 to 6
Outputs:
- attn_out: bfloat16 [48, 12288], P(('parts', 'head'), 'seq'), parts along dimension 0
There are 2 independent parts, one for each index of `parts`. A program takes and returns all parts, laid end to end along the dimension named above; an argument that names none is the same for every part. Nothing has to cross between parts.
Inputs may be any that keep to these rules, and one draw needn't show every extreme that they name: Sequence b holds lengths[b] cached tokens at positions 0 to lengths[b] - 1; its new token takes position lengths[b]. `key_cache`: positions at or past a sequence's length hold no data.
All inputs are finite; a program needn't handle non-finite values.
Results may differ from a plain program's by a relative error of at most 0.0075.
The roundings to bfloat16 on the way count: a program that leaves them out, or rounds other values in their place, can miss the bound.
Values may be sent and summed in bfloat16 or wider, within the bound.
No kernel may reach another device: no remote copies, remote signals or barrier semaphores. Data moves between devices by JAX's collectives and lax.ppermute only.
A program may use at most 64 MiB of HBM per device.

v0:
```python
import math
import jax
import jax.numpy as jnp
from jax import lax
from jax.sharding import PartitionSpec as P

D = 12288
EPSILON = 1e-05


def in_order(tiles, dim):
    tiles = jnp.moveaxis(tiles, 0, dim)
    dims = tiles.shape
    return tiles.reshape(*dims[:dim], dims[dim] * dims[dim + 1], *dims[dim + 2 :])


def sent_to_all(x, axis):
    copies = jnp.broadcast_to(x, (lax.axis_size(axis), *x.shape))
    return lax.all_to_all(copies, axis, split_axis=0, concat_axis=0, tiled=True)


def gather_directly(x, axis, dim):
    return in_order(sent_to_all(x, axis), dim)


def cut_along(x, dim, peers):
    before, after = (x.shape[:dim], x.shape[dim + 1 :])
    return jnp.moveaxis(x.reshape(*before, peers, -1, *after), dim, 0)


def summed_on_arrival(x, axis, dim):
    tiles = cut_along(x, dim, lax.axis_size(axis))
    arrived = lax.all_to_all(tiles, axis, split_axis=0, concat_axis=0, tiled=True)
    return arrived.sum(axis=0)


def in_one_piece(arrays, axis, dim, along):
    ends, at = ([], 0)
    for a in arrays[:-1]:
        at += a.shape[along]
        ends.append(at)
    both = jnp.concatenate(arrays, axis=along)
    return tuple(jnp.split(summed_on_arrival(both, axis, dim), ends, axis=along))


def in_one_piece_2(arrays, axis, dim, along):
    ends, at = ([], 0)
    for a in arrays[:-1]:
        at += a.shape[along]
        ends.append(at)
    both = jnp.concatenate(arrays, axis=along)
    return tuple(jnp.split(lax.all_gather(both, axis, axis=dim, tiled=True), ends, axis=along))


def side_by_side(arrays, axis, dim, along):
    widths = [math.prod(a.shape[along:]) for a in arrays]
    both = jnp.concatenate(
        [a.reshape(*a.shape[:along], w) for a, w in zip(arrays, widths)], axis=along
    )
    result = lax.all_gather(both, axis, axis=dim, tiled=True)
    tiles = jnp.split(result, [sum(widths[:k]) for k in range(1, len(widths))], axis=along)
    return tuple(
        (b.reshape(*result.shape[:along], *a.shape[along:]) for a, b in zip(arrays, tiles))
    )


def fold_blocks(totals, pieces):
    new_max = jnp.maximum(totals[0], jnp.max(pieces[0], axis=0))
    piece_factor = jnp.exp(pieces[0] - new_max[None])
    den_total = jnp.sum(piece_factor * pieces[1], axis=0)
    acc_total = jnp.sum(piece_factor[..., None] * pieces[2], axis=0)
    return (new_max, den_total, acc_total)


def local(hidden, norm_gain, w_query, w_key, w_value, w_out, lengths, key_cache, value_cache):
    batch_size, kv_local, block_len, head_size = key_cache.shape
    group_size = w_query.shape[1] // (kv_local * head_size)
    token_rows = gather_directly(hidden, "head", 0)
    widened = token_rows.astype(jnp.float32)
    square_local = jnp.sum(widened * widened, axis=1)
    scaled = (widened * norm_gain).astype(jnp.bfloat16)
    query_part = jnp.dot(scaled, w_query, preferred_element_type=jnp.float32)
    key_part = jnp.dot(scaled, w_key, preferred_element_type=jnp.float32)
    value_part = jnp.dot(scaled, w_value, preferred_element_type=jnp.float32)
    query_factor = float(head_size) ** (-0.5)
    square_tiled = jnp.broadcast_to(square_local[:, None], (batch_size, lax.axis_size("seq")))
    query_sum, key_sum, value_sum, norm_column = (
        summed_on_arrival(query_part, "seq", 1),
        *in_one_piece((key_part, value_part), "seq", 1, 0),
        summed_on_arrival(square_tiled, "seq", 1),
    )
    norm_total = norm_column[:, 0]
    inverse_rms = lax.rsqrt(norm_total / D + EPSILON)[:, None]
    queries = (query_sum * inverse_rms * query_factor).astype(jnp.bfloat16)
    new_keys = (key_sum * inverse_rms).astype(jnp.bfloat16)
    new_values = (value_sum * inverse_rms).astype(jnp.bfloat16)
    queries, new_keys, new_values = (
        lax.all_gather(queries, "seq", axis=1, tiled=True),
        *in_one_piece_2((new_keys, new_values), "seq", 1, 0),
    )
    grouped = queries.reshape(batch_size, kv_local, group_size, head_size)
    scores = jnp.einsum("bkgd,bkpd->bkgp", grouped, key_cache, preferred_element_type=jnp.float32)
    offset = lax.axis_index("seq") * block_len
    positions = offset + jnp.arange(block_len, dtype=jnp.int32)
    live_mask = (positions[None, :] < lengths[:, None])[:, None, None, :]
    block_max = jnp.max(jnp.where(live_mask, scores, -1e30), axis=-1)
    shifted = jnp.where(live_mask, scores - block_max[..., None], 0.0)
    weights = jnp.where(live_mask, jnp.exp(shifted), 0.0).astype(jnp.bfloat16)
    block_den = jnp.sum(weights.astype(jnp.float32), axis=-1)
    block_acc = jnp.einsum(
        "bkgp,bkpd->bkgd", weights, value_cache, preferred_element_type=jnp.float32
    )
    self_score = jnp.einsum(
        "oips,ois->oip",
        grouped,
        new_keys.reshape(batch_size, kv_local, head_size),
        preferred_element_type=jnp.float32,
    )
    initial = (
        jnp.full(block_max.shape, -1e30, jnp.float32),
        jnp.zeros(block_den.shape, jnp.float32),
        jnp.zeros(block_acc.shape, jnp.float32),
    )
    global_max, den_merged, acc_merged = fold_blocks(
        initial, side_by_side((block_max[None], block_den[None], block_acc[None]), "seq", 0, 4)
    )
    top_score = jnp.maximum(global_max, self_score)
    factors = jnp.exp(global_max - top_score)
    den_sum = den_merged * factors
    acc_sum = acc_merged * factors[..., None]
    own_weight = jnp.exp(self_score - top_score)
    denominator = den_sum + own_weight
    numerator = acc_sum + own_weight[..., None] * new_values.reshape(
        batch_size, kv_local, 1, head_size
    ).astype(jnp.float32)
    mixed = (
        (numerator / denominator[..., None])
        .astype(jnp.bfloat16)
        .reshape(batch_size, kv_local * group_size * head_size)
    )
    output = summed_on_arrival(jnp.dot(mixed, w_out, preferred_element_type=jnp.float32), "head", 0)
    return output.astype(jnp.bfloat16)


def solution(mesh):
    return jax.shard_map(
        local,
        mesh=mesh,
        in_specs=(
            P(("parts", "head"), "seq"),
            P("seq"),
            P("seq", "head"),
            P("seq", "head"),
            P("seq", "head"),
            P("head", "seq"),
            P("parts"),
            P("parts", "head", "seq", None),
            P("parts", "head", "seq", None),
        ),
        out_specs=P(("parts", "head"), "seq"),
        check_vma=False,
    )
```

profile of v0, /device:TPU:33, one launch (start us, length us, event | category | flops | bytes accessed | tf_op | source)
XLA Modules:
  0.0 357.4 jit_solution(9531133762320092091)
XLA Ops:
  6.5 0.0 copy-start
  6.6 0.0 copy-start.1
  6.6 1.4 broadcast_in_dim.49
  8.0 44.7 %all-to-all-start = ((bf16[8,3,384]{2,1,0:T(4,128)(2,1)}), bf16[8,3,384]{2,1,0:T(4,128)(2,1)S(1)}, u32[]{:S(2)}, u32[]{:S(2)}) async-start(bf16[8,3,384]{2,1,0:T(4,128)(2,1)} %broadcast_in_dim.49), calls=%async_computation | async-start | bytes 49152 | tf_op jit(solution)/shard_map/all_to_all | solution.py:19
  52.7 1.7 copy.66
  54.4 3.0 all-to-all-done
  57.4 0.8 multiply_reduce_fusion
  58.2 0.1 broadcast_in_dim.50
  58.3 0.6 transpose.24
  58.9 6.8 %all-to-all-start.2 = ((f32[32,24,1]{1,2,0:T(1,128)}), f32[32,24,1]{1,2,0:T(1,128)S(1)}, u32[]{:S(2)}, u32[]{:S(2)}) async-start(f32[32,24,1]{1,2,0:T(1,128)} %transpose.24), calls=%async_computation.2 | async-start | bytes 32768 | tf_op jit(solution)/shard_map/all_to_all | solution.py:33
  65.7 0.6 reshape.201
  66.3 0.0 copy-done.3
  66.3 1.6 convolution_bitcast_fusion
  67.8 1.1 reshape.206
  68.9 17.3 %all-to-all-done.2 = f32[32,24,1]{1,2,0:T(1,128)S(1)} async-done(((f32[32,24,1]{1,2,0:T(1,128)}), f32[32,24,1]{1,2,0:T(1,128)S(1)}, u32[]{:S(2)}, u32[]{:S(2)}) %all-to-all-start.2) | async-done | bytes 3104 | tf_op jit(solution)/shard_map/all_to_all | solution.py:33
  86.2 4.8 %all-to-all-start.1 = ((f32[32,1,1152]{2,1,0:T(1,128)}), f32[32,1,1152]{2,1,0:T(1,128)S(1)}, u32[]{:S(2)}, u32[]{:S(2)}) async-start(f32[32,1,1152]{2,1,0:T(1,128)} %reshape.206), calls=%async_computation.1 | async-start | bytes 294912 | tf_op jit(solution)/shard_map/all_to_all | solution.py:33
  91.0 0.1 all-gather.4.cloned.1.call-start
  91.1 0.7 broadcast_compare_fusion
  91.8 0.1 reduce_sum.74
  91.9 27.9 %all-to-all-done.1 = f32[32,1,1152]{2,1,0:T(1,128)S(1)} async-done(((f32[32,1,1152]{2,1,0:T(1,128)}), f32[32,1,1152]{2,1,0:T(1,128)S(1)}, u32[]{:S(2)}, u32[]{:S(2)}) %all-to-all-start.1) | async-done | bytes 147488 | tf_op jit(solution)/shard_map/all_to_all | solution.py:33
  119.8 0.5 broadcast.93
  120.3 1.0 reduce.10
  121.3 0.2 reshape.207
  121.6 0.1 fusion.13
  121.7 38.6 %all-gather = bf16[32,48,24]{1,2,0:T(8,128)(2,1)S(1)} all-gather(bf16[1,48,24]{1,2,0:T(8,128)(2,1)S(1)} %fusion.13), channel_id=1, replica_groups=mesh['parts'=2,'seq'=32,'head'=8] {'seq'}, dimensions={0}, use_global_device_ids=true | all-gather | bytes 76032 | tf_op jit(solution)/shard_map/all_gather | solution.py:98
  160.3 0.3 reshape.198
  160.5 0.1 reshape.190
  160.6 0.0 copy-done.1
  160.6 0.6 select_reduce_fusion
  161.2 0.2 convert_reduce_fusion
  161.5 0.0 copy-done.2
  161.5 0.4 convolution_bitcast_fusion.1
  161.9 0.3 copy.71
  162.1 0.3 copy.70
  162.4 0.3 pad_maximum_fusion
  162.7 0.9 copy.72
  163.6 0.1 all-gather.4.cloned.1.call-update
  163.6 0.0 copy-done.4
  163.6 1.0 fusion.14
  164.7 1.0 fusion.15
  165.8 0.1 copy.75
  165.9 0.1 reshape.208
  166.0 30.1 %all_to_all.25 = f32[32,1,192]{2,1,0:T(1,128)S(1)} all-to-all(f32[32,1,192]{2,1,0:T(1,128)S(1)} %reshape.208), channel_id=1, replica_groups=mesh['parts'=2,'seq'=32,'head'=8] {'seq'}, dimensions={0} | all-to-all | bytes 49152 | tf_op jit(solution)/shard_map/all_to_all | solution.py:33
  196.1 0.7 reduce.11
  196.8 0.1 reshape.209
  197.0 0.1 multiply_convert_fusion.6
  197.1 0.1 maximum_bitcast_fusion
  197.1 42.9 %all-gather.1 = bf16[32,4,48]{2,1,0:T(4,128)(2,1)S(1)} all-gather(bf16[1,4,48]{2,1,0:T(4,128)(2,1)S(1)} %maximum_bitcast_fusion), channel_id=1, replica_groups=mesh['parts'=2,'seq'=32,'head'=8] {'seq'}, dimensions={0}, use_global_device_ids=true | all-gather | bytes 12672 | tf_op jit(solution)/shard_map/all_gather | solution.py:52
  240.0 0.1 copy.76
  240.1 0.2 fusion.9
  240.3 0.1 copy.82
  240.4 61.3 %all-gather.4.cloned.1.call-done = f32[32,24,1,12,130]{4,1,3,2,0:T(8,128)} async-done(((f32[1,24,1,12,130]{4,1,3,2,0:T(8,128)}), f32[32,24,1,12,130]{4,1,3,2,0:T(8,128)}) %all-gather.4.cloned.1.call-update) | async-done | bytes 4792336 | tf_op jit(solution)/shard_map/all_gather | solution.py:60
  301.7 9.1 %fusion.18 = (f32[32,24,1,12,1]{4,1,3,2,0:T(8,128)}, f32[24,12]{0,1:T(8,128)S(1)}, f32[32,24,1,12,1]{4,1,3,2,0:T(8,128)}) fusion(f32[32,24,1,12,130]{4,1,3,2,0:T(8,128)} %all-gather.4.cloned.1.call-done), kind=kLoop, calls=%fused_computation.45 | loop fusion | flops 8928 | bytes 148608 | tf_op jit(solution)/shard_map/split | solution.py:61
  310.8 3.5 copy.88
  314.3 3.5 copy.87
  317.9 0.1 exponential_bitcast_fusion
  318.0 0.2 fusion.6
  318.2 0.2 copy.74
  318.4 5.1 %fusion = f32[24,12,128]{2,0,1:T(8,128)S(1)} fusion(f32[32,24,1,12,130]{4,1,3,2,0:T(8,128)} %all-gather.4.cloned.1.call-done, f32[32,24,12]{1,2,0:T(8,128)S(1)} %copy.74), kind=kLoop, calls=%fused_computation.1 | loop fusion | flops 2322432 | bytes 4902912 | tf_op jit(solution)/shard_map/reduce_sum | solution.py:71
  323.5 0.2 divide_convert_fusion
  323.7 0.0 copy-done
  323.7 0.3 fusion.1
  324.0 25.8 %all_to_all.26 = f32[8,3,384]{2,1,0:T(4,128)S(1)} all-to-all(f32[8,3,384]{2,1,0:T(4,128)S(1)} %copy.80), channel_id=1, replica_groups=mesh['parts'=2,'seq'=32,'head'=8] {'head'}, dimensions={0} | all-to-all | bytes 73728 | tf_op jit(solution)/shard_map/all_to_all | solution.py:33
  349.9 0.6 reduce_sum.79
  (16 shorter events, 0.3 us)
Async XLA Ops:
  6.5 317.2 %copy-start = (bf16[1536,384]{1,0:T(8,128)(2,1)S(1)}, bf16[1536,384]{1,0:T(8,128)(2,1)}, u32[]{:S(2)}) copy-start(bf16[1536,384]{1,0:T(8,128)(2,1)} %param.14) | copy-start | bytes 3538948
  6.6 154.1 %copy-start.1 = (bf16[24,1,128,128]{3,2,1,0:T(8,128)(2,1)S(1)}, bf16[24,1,128,128]{3,2,1,0:T(8,128)(2,1)}, u32[]{:S(2)}) copy-start(bf16[24,1,128,128]{3,2,1,0:T(8,128)(2,1)} %param.16) | copy-start | bytes 2359300
  8.0 49.4 %all-to-all-start = ((bf16[8,3,384]{2,1,0:T(4,128)(2,1)}), bf16[8,3,384]{2,1,0:T(4,128)(2,1)S(1)}, u32[]{:S(2)}, u32[]{:S(2)}) async-start(bf16[8,3,384]{2,1,0:T(4,128)(2,1)} %broadcast_in_dim.49), calls=%async_computation | async-start | bytes 49152 | tf_op jit(solution)/shard_map/all_to_all | solution.py:19
  57.4 8.9 %copy-start.3 = (bf16[8,3,384]{2,1,0:T(4,128)(2,1)}, bf16[8,3,384]{2,1,0:T(4,128)(2,1)S(1)}, u32[]{:S(2)}) copy-start(bf16[8,3,384]{2,1,0:T(4,128)(2,1)S(1)} %all-to-all-done) | copy-start | bytes 55300
  58.9 27.3 %all-to-all-start.2 = ((f32[32,24,1]{1,2,0:T(1,128)}), f32[32,24,1]{1,2,0:T(1,128)S(1)}, u32[]{:S(2)}, u32[]{:S(2)}) async-start(f32[32,24,1]{1,2,0:T(1,128)} %transpose.24), calls=%async_computation.2 | async-start | bytes 32768 | tf_op jit(solution)/shard_map/all_to_all | solution.py:33
  67.8 93.6 %copy-start.2 = (bf16[24,1,128,128]{3,2,1,0:T(8,128)(2,1)S(1)}, bf16[24,1,128,128]{3,2,1,0:T(8,128)(2,1)}, u32[]{:S(2)}) copy-start(bf16[24,1,128,128]{3,2,1,0:T(8,128)(2,1)} %param.17) | copy-start | bytes 2359300
  68.9 94.7 %copy-start.4 = (bf16[8,3,384]{2,1,0:T(4,128)(2,1)S(1)}, bf16[8,3,384]{2,1,0:T(4,128)(2,1)}, u32[]{:S(2)}) copy-start(bf16[8,3,384]{2,1,0:T(4,128)(2,1)} %copy-done.3) | copy-start | bytes 55300
  86.2 33.6 %all-to-all-start.1 = ((f32[32,1,1152]{2,1,0:T(1,128)}), f32[32,1,1152]{2,1,0:T(1,128)S(1)}, u32[]{:S(2)}, u32[]{:S(2)}) async-start(f32[32,1,1152]{2,1,0:T(1,128)} %reshape.206), calls=%async_computation.1 | async-start | bytes 294912 | tf_op jit(solution)/shard_map/all_to_all | solution.py:33
  91.0 210.7 %all-gather.4.cloned.1.call-start = ((), (), s32[]{:S(2)}) async-start(), calls=%async_computation.5 | async-start | bytes 9732096 | tf_op jit(solution)/shard_map/all_gather | solution.py:60
Sparse Core Ops, SparseCore 0:
  163.7 137.9 all-gather.3
where the time goes:
time: 358 us; the launch traced here: 357 us
  blocking collectives  137 us (38%)
  waiting for transfers between devices  110 us (31%)
  starting transfers between devices  56.3 us (16%)
  other arithmetic  19.4 us (5%)
  local copies, waits for them, and re-layouts  15.8 us (4%)
  between operations  13.7 us (4%)
  matrix products  5.05 us (1%)
    all_gather x1, waiting for transfers between devices, side_by_side(): result = lax.all_gather(both, axis, axis=dim, tiled=True)  61.3 us
    all_to_all x2, blocking collectives, summed_on_arrival(): lax.all_to_all(tiles, axis, split_axis=0, concat_axis=0, tiled=True)  56 us
    all_to_all x2, waiting for transfers between devices, summed_on_arrival(): lax.all_to_all(tiles, axis, split_axis=0, concat_axis=0, tiled=True)  45.3 us
    all_to_all x1, starting transfers between devices, sent_to_all(): return lax.all_to_all(copies, axis, split_axis=0, concat_axis=0, tiled=True)  44.7 us
    all_gather x1, blocking collectives, in_one_piece_2(): lax.all_gather(both, axis, axis=dim, tiled=True)  42.9 us
    all_gather x1, blocking collectives, local(): lax.all_gather(queries, 'seq', axis=1, tiled=True)  38.6 us
    all_to_all x2, starting transfers between devices, summed_on_arrival(): lax.all_to_all(tiles, axis, split_axis=0, concat_axis=0, tiled=True)  11.5 us
    unnamed x19, local copies, waits for them, and re-layouts  10.6 us
  transfers between devices with their start and end apart: 4, of which 4 were waited for; matrix products, arithmetic and copies ran while one was open for 3% of the time, Pallas kernels for 0%

commit v1 on v0

--- a/solution.py
+++ b/solution.py
@@ -6,6 +6,11 @@
 
 D = 12288
 EPSILON = 1e-05
+
+
+def plan_hubs_by_axis(block_in):
+    reply = lax.all_gather(block_in, axis_name="seq")
+    return jnp.concatenate(reply, axis=1)
 
 
 def in_order(tiles, dim):
@@ -95,7 +100,7 @@
     new_keys = (key_sum * inverse_rms).astype(jnp.bfloat16)
     new_values = (value_sum * inverse_rms).astype(jnp.bfloat16)
     queries, new_keys, new_values = (
-        lax.all_gather(queries, "seq", axis=1, tiled=True),
+        plan_hubs_by_axis(queries),
         *in_one_piece_2((new_keys, new_values), "seq", 1, 0),
     )
     grouped = queries.reshape(batch_size, kv_local, group_size, head_size)

time: 358 us -> 358 us (level)
    unnamed x19 -> x22, local copies, waits for them, and re-layouts: 10.6 us -> 10.3 us
  transfers between devices with their start and end apart: 4 -> 4, of which waited for: 4 -> 4; matrix products, arithmetic and copies ran while one was open for 3% -> 2% of each run, Pallas kernels for 0% -> 0%
where the time goes in v1:
time: 358 us
  blocking collectives  136 us (38%)
  waiting for transfers between devices  112 us (31%)
  starting transfers between devices  56.3 us (16%)
  other arithmetic  19.4 us (5%)
  local copies, waits for them, and re-layouts  15.6 us (4%)
  between operations  13.7 us (4%)
  matrix products  4.36 us (1%)
    all_gather x1, waiting for transfers between devices, side_by_side(): result = lax.all_gather(both, axis, axis=dim, tiled=True)  63.6 us
    all_to_all x2, blocking collectives, summed_on_arrival(): lax.all_to_all(tiles, axis, split_axis=0, concat_axis=0, tiled=True)  55.8 us
    all_to_all x2, waiting for transfers between devices, summed_on_arrival(): lax.all_to_all(tiles, axis, split_axis=0, concat_axis=0, tiled=True)  45.3 us
    all_to_all x1, starting transfers between devices, sent_to_all(): return lax.all_to_all(copies, axis, split_axis=0, concat_axis=0, tiled=True)  44.7 us
    all_gather x1, blocking collectives, in_one_piece_2(): lax.all_gather(both, axis, axis=dim, tiled=True)  41.9 us
    all_gather x1, blocking collectives, plan_hubs_by_axis(): reply = lax.all_gather(block_in, axis_name='seq')  38.6 us
    all_to_all x2, starting transfers between devices, summed_on_arrival(): lax.all_to_all(tiles, axis, split_axis=0, concat_axis=0, tiled=True)  11.5 us
    unnamed x22, local copies, waits for them, and re-layouts  10.3 us
  transfers between devices with their start and end apart: 4, of which 4 were waited for; matrix products, arithmetic and copies ran while one was open for 2% of the time, Pallas kernels for 0%

profile of v1, /device:TPU:33, one launch (start us, length us, event | category | flops | bytes accessed | tf_op | source)
XLA Modules:
  0.0 357.7 jit_solution(17813467417402396910)
XLA Ops:
  6.5 0.0 copy-start
  6.6 1.4 broadcast_in_dim.49
  8.0 44.7 %all-to-all-start = ((bf16[8,3,384]{2,1,0:T(4,128)(2,1)}), bf16[8,3,384]{2,1,0:T(4,128)(2,1)S(1)}, u32[]{:S(2)}, u32[]{:S(2)}) async-start(bf16[8,3,384]{2,1,0:T(4,128)(2,1)} %broadcast_in_dim.49), calls=%async_computation | async-start | bytes 49152 | tf_op jit(solution)/shard_map/all_to_all | solution.py:24
  52.7 1.7 copy.65
  54.4 3.0 all-to-all-done
  57.4 0.8 multiply_reduce_fusion
  58.2 0.1 broadcast_in_dim.50
  58.3 0.6 transpose.24
  58.9 6.8 %all-to-all-start.2 = ((f32[32,24,1]{1,2,0:T(1,128)}), f32[32,24,1]{1,2,0:T(1,128)S(1)}, u32[]{:S(2)}, u32[]{:S(2)}) async-start(f32[32,24,1]{1,2,0:T(1,128)} %transpose.24), calls=%async_computation.2 | async-start | bytes 32768 | tf_op jit(solution)/shard_map/all_to_all | solution.py:38
  65.7 0.6 reshape.234
  66.3 0.0 copy-done.2
  66.3 1.6 convolution_bitcast_fusion
  67.8 0.0 copy-start.6
  67.9 0.0 copy-start.5
  67.9 1.0 reshape.239
  68.9 17.3 %all-to-all-done.2 = f32[32,24,1]{1,2,0:T(1,128)S(1)} async-done(((f32[32,24,1]{1,2,0:T(1,128)}), f32[32,24,1]{1,2,0:T(1,128)S(1)}, u32[]{:S(2)}, u32[]{:S(2)}) %all-to-all-start.2) | async-done | bytes 3104 | tf_op jit(solution)/shard_map/all_to_all | solution.py:38
  86.2 4.8 %all-to-all-start.1 = ((f32[32,1,1152]{2,1,0:T(1,128)}), f32[32,1,1152]{2,1,0:T(1,128)S(1)}, u32[]{:S(2)}, u32[]{:S(2)}) async-start(f32[32,1,1152]{2,1,0:T(1,128)} %reshape.239), calls=%async_computation.1 | async-start | bytes 294912 | tf_op jit(solution)/shard_map/all_to_all | solution.py:38
  91.0 0.1 all-gather.3.cloned.1.call-start
  91.1 0.7 broadcast_compare_fusion
  91.8 0.1 reduce_sum.77
  91.9 27.9 %all-to-all-done.1 = f32[32,1,1152]{2,1,0:T(1,128)S(1)} async-done(((f32[32,1,1152]{2,1,0:T(1,128)}), f32[32,1,1152]{2,1,0:T(1,128)S(1)}, u32[]{:S(2)}, u32[]{:S(2)}) %all-to-all-start.1) | async-done | bytes 147488 | tf_op jit(solution)/shard_map/all_to_all | solution.py:38
  119.8 0.5 broadcast.115
  120.3 1.0 reduce.10
  121.3 0.2 reshape.240
  121.6 0.1 fusion.10
  121.7 38.6 %all_gather.10 = bf16[32,24,48]{2,1,0:T(8,128)(2,1)S(1)} all-gather(bf16[1,24,48]{2,1,0:T(8,128)(2,1)S(1)} %fusion.10), channel_id=1, replica_groups=mesh['parts'=2,'seq'=32,'head'=8] {'seq'}, dimensions={0}, use_global_device_ids=true | all-gather | bytes 76032 | tf_op jit(solution)/shard_map/all_gather | solution.py:12
  160.3 0.2 reshape.225
  160.5 0.0 copy-done.1
  160.5 0.6 select_reduce_fusion
  161.0 0.2 convert_reduce_fusion
  161.3 1.5 convolution_bitcast_fusion.1
  162.8 0.3 copy.70
  163.1 0.3 copy.69
  163.3 0.3 pad_maximum_fusion
  163.6 0.9 copy.71
  164.5 0.1 all-gather.3.cloned.1.call-update
  164.6 0.0 copy-done.3
  164.6 0.0 copy-done.4
  164.6 0.1 fusion.15
  164.8 0.0 copy-done.5
  164.8 0.1 fusion.16
  164.9 0.1 copy.74
  165.0 0.1 reshape.241
  165.2 30.1 %all_to_all.25 = f32[32,1,192]{2,1,0:T(1,128)S(1)} all-to-all(f32[32,1,192]{2,1,0:T(1,128)S(1)} %reshape.241), channel_id=1, replica_groups=mesh['parts'=2,'seq'=32,'head'=8] {'seq'}, dimensions={0} | all-to-all | bytes 49152 | tf_op jit(solution)/shard_map/all_to_all | solution.py:38
  195.3 0.7 reduce.11
  196.0 0.1 reshape.242
  196.1 0.1 multiply_convert_fusion.5
  196.2 0.1 maximum_bitcast_fusion
  196.3 41.9 %all-gather = bf16[32,4,48]{2,1,0:T(4,128)(2,1)S(1)} all-gather(bf16[1,4,48]{2,1,0:T(4,128)(2,1)S(1)} %maximum_bitcast_fusion), channel_id=1, replica_groups=mesh['parts'=2,'seq'=32,'head'=8] {'seq'}, dimensions={0}, use_global_device_ids=true | all-gather | bytes 12672 | tf_op jit(solution)/shard_map/all_gather | solution.py:57
  238.3 0.1 copy.75
  238.3 0.2 fusion.11
  238.5 0.1 copy.81
  238.6 63.6 %all-gather.3.cloned.1.call-done = f32[32,24,1,12,130]{4,1,3,2,0:T(8,128)} async-done(((f32[1,24,1,12,130]{4,1,3,2,0:T(8,128)}), f32[32,24,1,12,130]{4,1,3,2,0:T(8,128)}) %all-gather.3.cloned.1.call-update) | async-done | bytes 4792336 | tf_op jit(solution)/shard_map/all_gather | solution.py:65
  302.2 9.1 %fusion.19 = (f32[32,24,1,12,1]{4,1,3,2,0:T(8,128)}, f32[24,12]{0,1:T(8,128)S(1)}, f32[32,24,1,12,1]{4,1,3,2,0:T(8,128)}) fusion(f32[32,24,1,12,130]{4,1,3,2,0:T(8,128)} %all-gather.3.cloned.1.call-done), kind=kLoop, calls=%fused_computation.46 | loop fusion | flops 8928 | bytes 148608 | tf_op jit(solution)/shard_map/split | solution.py:66
  311.3 3.5 copy.87
  314.8 3.5 copy.86
  318.3 0.1 exponential_bitcast_fusion
  318.4 0.2 fusion.6
  318.6 0.2 copy.73
  318.8 5.1 %fusion = f32[24,12,128]{2,0,1:T(8,128)S(1)} fusion(f32[32,24,1,12,130]{4,1,3,2,0:T(8,128)} %all-gather.3.cloned.1.call-done, f32[32,24,12]{1,2,0:T(8,128)S(1)} %copy.73), kind=kLoop, calls=%fused_computation.1 | loop fusion | flops 2322432 | bytes 4902912 | tf_op jit(solution)/shard_map/reduce_sum | solution.py:76
  323.9 0.2 divide_convert_fusion
  324.2 0.3 fusion.1
  324.5 25.7 %all_to_all.26 = f32[8,3,384]{2,1,0:T(4,128)S(1)} all-to-all(f32[8,3,384]{2,1,0:T(4,128)S(1)} %copy.79), channel_id=1, replica_groups=mesh['parts'=2,'seq'=32,'head'=8] {'head'}, dimensions={0} | all-to-all | bytes 73728 | tf_op jit(solution)/shard_map/all_to_all | solution.py:38
  350.2 0.6 reduce_sum.82
  (19 shorter events, 0.3 us)
Async XLA Ops:
  6.5 317.6 %copy-start = (bf16[1536,384]{1,0:T(8,128)(2,1)S(1)}, bf16[1536,384]{1,0:T(8,128)(2,1)}, u32[]{:S(2)}) copy-start(bf16[1536,384]{1,0:T(8,128)(2,1)} %param.14) | copy-start | bytes 3538948
  6.6 153.9 %copy-start.1 = (bf16[24,1,128,128]{3,2,1,0:T(8,128)(2,1)S(1)}, bf16[24,1,128,128]{3,2,1,0:T(8,128)(2,1)}, u32[]{:S(2)}) copy-start(bf16[24,1,128,128]{3,2,1,0:T(8,128)(2,1)} %param.16) | copy-start | bytes 2359300
  8.0 49.4 %all-to-all-start = ((bf16[8,3,384]{2,1,0:T(4,128)(2,1)}), bf16[8,3,384]{2,1,0:T(4,128)(2,1)S(1)}, u32[]{:S(2)}, u32[]{:S(2)}) async-start(bf16[8,3,384]{2,1,0:T(4,128)(2,1)} %broadcast_in_dim.49), calls=%async_computation | async-start | bytes 49152 | tf_op jit(solution)/shard_map/all_to_all | solution.py:24
  57.4 8.9 %copy-start.2 = (bf16[8,3,384]{2,1,0:T(4,128)(2,1)}, bf16[8,3,384]{2,1,0:T(4,128)(2,1)S(1)}, u32[]{:S(2)}) copy-start(bf16[8,3,384]{2,1,0:T(4,128)(2,1)S(1)} %all-to-all-done) | copy-start | bytes 55300
  58.9 27.3 %all-to-all-start.2 = ((f32[32,24,1]{1,2,0:T(1,128)}), f32[32,24,1]{1,2,0:T(1,128)S(1)}, u32[]{:S(2)}, u32[]{:S(2)}) async-start(f32[32,24,1]{1,2,0:T(1,128)} %transpose.24), calls=%async_computation.2 | async-start | bytes 32768 | tf_op jit(solution)/shard_map/all_to_all | solution.py:38
  67.8 96.7 %copy-start.3 = (bf16[8,3,384]{2,1,0:T(4,128)(2,1)S(1)}, bf16[8,3,384]{2,1,0:T(4,128)(2,1)}, u32[]{:S(2)}) copy-start(bf16[8,3,384]{2,1,0:T(4,128)(2,1)} %copy-done.2) | copy-start | bytes 55300
  67.8 96.8 %copy-start.4 = (bf16[384,128]{1,0:T(8,128)(2,1)S(1)}, bf16[384,128]{1,0:T(8,128)(2,1)}, u32[]{:S(2)}) copy-start(bf16[384,128]{1,0:T(8,128)(2,1)} %param.13) | copy-start | bytes 294916
  67.8 96.8 %copy-start.6 = (f32[384]{0:T(512)S(1)}, f32[384]{0:T(512)}, u32[]{:S(2)}) copy-start(f32[384]{0:T(512)} %param.10) | copy-start | bytes 4612
  67.9 96.9 %copy-start.5 = (bf16[384,128]{1,0:T(8,128)(2,1)S(1)}, bf16[384,128]{1,0:T(8,128)(2,1)}, u32[]{:S(2)}) copy-start(bf16[384,128]{1,0:T(8,128)(2,1)} %param.12) | copy-start | bytes 294916
  86.2 33.6 %all-to-all-start.1 = ((f32[32,1,1152]{2,1,0:T(1,128)}), f32[32,1,1152]{2,1,0:T(1,128)S(1)}, u32[]{:S(2)}, u32[]{:S(2)}) async-start(f32[32,1,1152]{2,1,0:T(1,128)} %reshape.239), calls=%async_computation.1 | async-start | bytes 294912 | tf_op jit(solution)/shard_map/all_to_all | solution.py:38
  91.0 211.2 %all-gather.3.cloned.1.call-start = ((), (), s32[]{:S(2)}) async-start(), calls=%async_computation.5 | async-start | bytes 9732096 | tf_op jit(solution)/shard_map/all_gather | solution.py:65
Sparse Core Ops, SparseCore 0:
  164.7 137.4 all-gather.2
